TPU v7x, 32 devices: a whole 2x2x4 slice. The times are simulated.
32 devices in a mesh: hot: 8 (over z, y), cold: 4 (over x, core).
Axes of the slice: x: 2, y: 2, z: 4, core: 2. Of those that a mesh axis runs over, the one named last changes fastest.
Arguments:
- tokens: bfloat16 [64, 8192], replicated, may hold values from -6 to 6
- norm_gain: float32 [8192], replicated, may hold values from 0.1 to 1.9
- hot_gate: bfloat16 [512, 8192], P(('hot', 'cold')), may hold values from -0.0625 to 0.0625
- hot_up: bfloat16 [512, 8192], P(('hot', 'cold')), may hold values from -0.0625 to 0.0625
- hot_down: bfloat16 [512, 8192], P(('hot', 'cold')), may hold values from -0.09375 to 0.09375
- hot_index: int32 [512], replicated, may hold values from 0 to 14335, as said below
- cold_gate: bfloat16 [8192, 14336], P('hot', 'cold'), may hold values from -0.0625 to 0.0625
- cold_up: bfloat16 [8192, 14336], P('hot', 'cold'), may hold values from -0.0625 to 0.0625
- cold_down: bfloat16 [14336, 8192], P('cold', 'hot'), may hold values from -0.0625 to 0.0625
- block_mask: int32 [64, 112], P(None, 'cold'), may hold values from 0 to 1, as said below
Outputs:
- ffn_out: bfloat16 [64, 8192], P(None, ('hot', 'cold'))
Inputs may be any that keep to these rules, and one draw needn't show every extreme that they name: `hot_index`: distinct hidden units. `block_mask`: in each run of 28 blocks held by one index of cold, at most 14 blocks are active for any sequence, and some index reaches exactly 14.
All inputs are finite; a program needn't handle non-finite values.
Results may differ from a plain program's by a relative error of at most 0.0065.
Values may be sent and summed in bfloat16 or wider, within the bound.
No kernel may reach another device: no remote copies, remote signals or barrier semaphores. Data moves between devices by JAX's collectives and lax.ppermute only.
A program may use at most 64 MiB of HBM per device.

v0:
```python
import jax
import jax.numpy as jnp
from jax import lax
from jax.sharding import PartitionSpec as P

UNITS = 14336


def on_device(
    tokens,
    norm_gain,
    hot_gate,
    hot_up,
    hot_down,
    hot_index,
    cold_gate,
    cold_up,
    cold_down,
    block_mask,
):
    values = tokens.astype(jnp.float32)
    scale = lax.rsqrt(jnp.mean(values * values, axis=1, keepdims=True) + 1e-05)
    normed = (values * scale * norm_gain[None, :]).astype(jnp.bfloat16)
    dims = (((1,), (1,)), ((), ()))
    gate_hot = lax.dot_general(normed, hot_gate, dims, preferred_element_type=jnp.float32)
    up_hot = lax.dot_general(normed, hot_up, dims, preferred_element_type=jnp.float32)
    hidden_hot = (jax.nn.silu(gate_hot) * up_hot).astype(jnp.bfloat16)
    feat_rows = cold_gate.shape[0]
    unit_count = cold_gate.shape[1]
    blocks_here = block_mask.shape[1]
    block = unit_count // blocks_here
    seqs = tokens.shape[0]
    is_hot = jnp.zeros((UNITS,), jnp.float32).at[hot_index].set(1.0)
    local_hot = lax.dynamic_slice_in_dim(is_hot, lax.axis_index("cold") * unit_count, unit_count)
    normed_part = lax.dynamic_slice_in_dim(normed, lax.axis_index("hot") * feat_rows, feat_rows, 1)
    gate_w, up_w, down_w = (cold_gate, cold_up, cold_down)
    seq_live = block_mask.astype(jnp.float32)
    unit_live = (1.0 - local_hot).reshape(blocks_here, block)
    live = (seq_live[:, :, None] * unit_live[None, :, :]).reshape(seqs, unit_count)
    gate_part = jnp.dot(normed_part, gate_w, preferred_element_type=jnp.float32)
    up_part = jnp.dot(normed_part, up_w, preferred_element_type=jnp.float32)
    gate_cold, up_cold = lax.psum((gate_part, up_part), "hot")
    hidden_cold = (jax.nn.silu(gate_cold) * up_cold * live).astype(jnp.bfloat16)
    out_cold = jnp.dot(hidden_cold, down_w, preferred_element_type=jnp.float32)
    down_cols = lax.all_to_all(hot_down, ("hot", "cold"), split_axis=1, concat_axis=0, tiled=True)
    hidden_all = lax.all_gather(hidden_hot, ("hot", "cold"), axis=1, tiled=True)
    hot_total = jnp.dot(hidden_all, down_cols, preferred_element_type=jnp.float32)
    cold_total = lax.psum_scatter(out_cold, "cold", scatter_dimension=1, tiled=True)
    total = hot_total + cold_total
    return total.astype(jnp.bfloat16)


def solution(mesh):
    in_specs = (
        P(),
        P(),
        P(("hot", "cold"), None),
        P(("hot", "cold"), None),
        P(("hot", "cold"), None),
        P(),
        P("hot", "cold"),
        P("hot", "cold"),
        P("cold", "hot"),
        P(None, "cold"),
    )
    out_specs = P(None, ("hot", "cold"))
    return jax.shard_map(
        on_device, mesh=mesh, in_specs=in_specs, out_specs=out_specs, check_vma=False
    )
```

profile of v0, /device:TPU:0, one launch (start us, length us, event | category | flops | bytes accessed | tf_op | source)
XLA Modules:
  0.0 177.9 jit_solution(3256755410243305480)
XLA Ops:
  6.5 0.0 copy-start
  6.5 0.0 all-reduce.3.cloned.1.call-start
  6.5 1.6 fusion
  8.1 0.0 slice-start
  8.1 1.7 fusion.2
  9.8 0.0 slice-start.1
  9.8 5.6 %fusion.11 = f32[64,3584]{1,0:T(8,128)} fusion(bf16[1024,3584]{1,0:T(8,128)(2,1)} %param.17, bf16[64,8192]{1,0:T(8,128)(2,1)S(1)} %fusion.2, s32[]{:T(128)S(6)} %select_n.9), kind=kOutput, calls=%fused_computation.17 | convolution fusion | flops 469762048 | bytes 8388612 | tf_op jit(solution)/shard_map/dot_general | solution.py:41
  15.4 0.0 slice-done
  15.4 0.0 slice-done.1
  15.4 0.0 copy-start.2
  15.4 0.0 copy-start.3
  15.5 0.0 copy-start.4
  15.5 2.3 %fusion.13 = f32[64,3584]{1,0:T(8,128)} fusion(bf16[1024,3584]{1,0:T(8,128)(2,1)S(1)} %bitcast.25, bf16[64,8192]{1,0:T(8,128)(2,1)S(1)} %fusion.2, s32[]{:T(128)S(6)} %select_n.9), kind=kOutput, calls=%fused_computation.19 | convolution fusion | flops 469762048 | bytes 8388612 | tf_op jit(solution)/shard_map/dot_general | solution.py:40
  17.8 0.0 all-reduce.3.cloned.1.call-update
  17.8 0.0 copy-start.1
  17.8 0.0 copy-done.2
  17.8 0.7 copy.22
  18.5 7.3 %all-to-all-start = ((bf16[16,32,256]{2,0,1:T(8,128)(2,1)}), bf16[16,32,256]{2,0,1:T(8,128)(2,1)S(1)}, u32[]{:S(2)}, u32[]{:S(2)}) async-start(bf16[16,32,256]{2,0,1:T(8,128)(2,1)} %bitcast.23), calls=%async_computation | async-start | bytes 524288 | tf_op jit(solution)/shard_map/all_to_all | solution.py:45
  25.9 0.0 reduce-scatter.2.cloned.1.call-start
  25.9 0.0 copy-done.3
  26.0 0.1 copy.16
  26.0 0.0 copy-done.4
  26.1 2.5 %scatter_custom_fusion = f32[14336]{0:T(1024)S(1)} fusion(s32[512]{0:T(512)S(1)} %compare_select_fusion, f32[512]{0:T(512)S(1)} %broadcast.20, f32[]{:T(128)} %constant.12.clone.1), kind=kCustom, calls=%fused_computation.21 | custom fusion | bytes 57348 | tf_op jit(solution)/shard_map/scatter | solution.py:33
  28.6 0.1 dynamic-slice_subtract_fusion
  28.6 93.3 %all-reduce.3.cloned.1.call-done = (f32[64,3584]{1,0:T(8,128)}, f32[64,3584]{1,0:T(8,128)}) async-done(((f32[64,3584]{1,0:T(8,128)}, f32[64,3584]{1,0:T(8,128)}), (f32[64,3584]{1,0:T(8,128)}, f32[64,3584]{1,0:T(8,128)})) %all-reduce.3.cloned.1.call-update) | async-done | bytes 1835024 | tf_op jit(solution)/shard_map/psum | solution.py:42
  121.9 0.3 mul.68
  122.3 6.2 %fusion.7 = f32[64,1024]{1,0:T(8,128)} fusion(bf16[3584,1024]{1,0:T(8,128)(2,1)} %param.18, f32[8,8,28,128]{3,2,1,0:T(8,128)S(1)} %bitcast.26, f32[64,3584]{1,0:T(8,128)} %get-tuple-element.5, f32[64,3584]{1,0:T(8,128)} %get-tuple-element.6, f32[3584]{0:T(1024)S(1)} %dynamic-slice_subtract_fusion), kind=kOutput, calls=%fused_computation.13 | convolution fusion | flops 471597056 | bytes 10369024 | tf_op jit(solution)/shard_map/dot_general | solution.py:44
  128.5 0.0 reduce-scatter.2.cloned.1.call-update
  128.5 0.0 copy-done
  128.5 0.4 fusion.20
  128.9 0.0 copy-done.1
  128.9 0.4 fusion.4
  129.3 40.1 %all_gather.3 = bf16[64,512]{0,1:T(8,128)(2,1)S(1)} all-gather(bf16[64,16]{0,1:T(8,128)(2,1)S(1)} %fusion.4), channel_id=1, replica_groups=mesh['hot'=8,'cold'=4] {'hot','cold'}, dimensions={1}, use_global_device_ids=true | all-gather | bytes 67584 | tf_op jit(solution)/shard_map/all_gather | solution.py:46
  169.4 0.0 all-to-all-done
  169.4 0.0 reduce-scatter.2.cloned.1.call-done
  169.4 1.7 fusion.3
  (5 shorter events, 0.0 us)
Async XLA Ops:
  6.5 122.0 %copy-start = (bf16[16,8192]{1,0:T(8,128)(2,1)S(1)}, bf16[16,8192]{1,0:T(8,128)(2,1)}, u32[]{:S(2)}) copy-start(bf16[16,8192]{1,0:T(8,128)(2,1)} %param.12) | copy-start | bytes 786436
  6.5 115.4 %all-reduce.3.cloned.1.call-start = ((), (), s32[]{:S(2)}) async-start(), calls=%async_computation.3 | async-start | bytes 3670016 | tf_op jit(solution)/shard_map/psum | solution.py:42
  8.1 7.3 %slice-start = ((s8[7340032]{0:T(1024)(128)(4,1)}), s8[4194304]{0:T(1024)(128)(4,1)S(1)}, s32[]{:S(2)}) async-start(s8[7340032]{0:T(1024)(128)(4,1)} %bitcast.24), calls=%async_computation.4 | async-start | bytes 8388608
  9.8 5.6 %slice-start.1 = ((s8[7340032]{0:T(1024)(128)(4,1)}), s8[3145728]{0:T(1024)(128)(4,1)S(1)}, s32[]{:S(2)}) async-start(s8[7340032]{0:T(1024)(128)(4,1)} %bitcast.24), calls=%async_computation.5 | async-start | bytes 6291456
  15.4 2.4 %copy-start.2 = (bf16[16,8192]{1,0:T(8,128)(2,1)S(1)}, bf16[16,8192]{1,0:T(8,128)(2,1)}, u32[]{:S(2)}) copy-start(bf16[16,8192]{1,0:T(8,128)(2,1)} %param.14) | copy-start | bytes 786436
  15.4 10.5 %copy-start.3 = (s32[64,28]{0,1:T(8,128)S(1)}, s32[64,28]{0,1:T(8,128)}, u32[]{:S(2)}) copy-start(s32[64,28]{0,1:T(8,128)} %param.19) | copy-start | bytes 21508
  15.5 10.6 %copy-start.4 = (s32[512]{0:T(512)S(1)}, s32[512]{0:T(512)}, u32[]{:S(2)}) copy-start(s32[512]{0:T(512)} %param.15) | copy-start | bytes 6148
  17.8 111.1 %copy-start.1 = (bf16[16,8192]{1,0:T(8,128)(2,1)S(1)}, bf16[16,8192]{1,0:T(8,128)(2,1)}, u32[]{:S(2)}) copy-start(bf16[16,8192]{1,0:T(8,128)(2,1)} %param.13) | copy-start | bytes 786436
  18.5 150.8 %all-to-all-start = ((bf16[16,32,256]{2,0,1:T(8,128)(2,1)}), bf16[16,32,256]{2,0,1:T(8,128)(2,1)S(1)}, u32[]{:S(2)}, u32[]{:S(2)}) async-start(bf16[16,32,256]{2,0,1:T(8,128)(2,1)} %bitcast.23), calls=%async_computation | async-start | bytes 524288 | tf_op jit(solution)/shard_map/all_to_all | solution.py:45
  25.9 143.5 %reduce-scatter.2.cloned.1.call-start = ((), (), s32[]{:S(2)}) async-start(), calls=%async_computation.2 | async-start | bytes 327680 | tf_op jit(solution)/shard_map/reduce_scatter | solution.py:48
Sparse Core Ops, SparseCore 0:
  17.9 103.9 all-reduce.2
  128.6 19.6 reduce-scatter.1
where the time goes:
time: 178 us
  waiting for transfers between devices  93.3 us (52%)
  blocking collectives  40.1 us (23%)
  matrix products  16.5 us (9%)
  between operations  13.5 us (8%)
  starting transfers between devices  7.37 us (4%)
  local copies, waits for them, and re-layouts  3.65 us (2%)
  other arithmetic  3.35 us (2%)
    psum x1, waiting for transfers between devices, on_device(): gate_cold, up_cold = lax.psum((gate_part, up_part), 'hot')  93.3 us
    all_gather x1, blocking collectives, on_device(): hidden_all = lax.all_gather(hidden_hot, ('hot', 'cold'), axis=1, tiled=True)  40.1 us
    all_to_all x1, starting transfers between devices, on_device(): lax.all_to_all(hot_down, ('hot', 'cold'), split_axis=1, concat_axis=0, ti...  7.32 us
    dot_general x1, matrix products, on_device(): out_cold = jnp.dot(hidden_cold, down_w, preferred_element_type=jnp.float32)  6.19 us
    dot_general x1, matrix products, on_device(): up_part = jnp.dot(normed_part, up_w, preferred_element_type=jnp.float32)  5.59 us
  transfers between devices with their start and end apart: 3, of which 1 were waited for; matrix products, arithmetic and copies ran while one was open for 6% of the time, Pallas kernels for 0%

commit v1 on v0

--- a/solution.py
+++ b/solution.py
@@ -1,9 +1,25 @@
+import functools
 import jax
 import jax.numpy as jnp
 from jax import lax
 from jax.sharding import PartitionSpec as P
 
 UNITS = 14336
+
+
+def start_the_ends(patch, comm_axis):
+    before, seen_now = (lax.axis_size(comm_axis), lax.axis_index(comm_axis))
+    x_new, g_now = (patch, 1)
+    while g_now < before:
+        o_now = lax.ppermute(x_new, comm_axis, [(h, h ^ g_now) for h in range(before)])
+        far_arr = jnp.concatenate([x_new, o_now], 1)
+        met_up = jnp.concatenate([o_now, x_new], 1)
+        x_new = jnp.where(seen_now & g_now == 0, far_arr, met_up)
+        g_now = 2 * g_now
+    return x_new
+
+
+show_rails_by_axis = functools.partial(start_the_ends, comm_axis=("hot", "cold"))
 
 
 def on_device(
@@ -43,7 +59,7 @@
     hidden_cold = (jax.nn.silu(gate_cold) * up_cold * live).astype(jnp.bfloat16)
     out_cold = jnp.dot(hidden_cold, down_w, preferred_element_type=jnp.float32)
     down_cols = lax.all_to_all(hot_down, ("hot", "cold"), split_axis=1, concat_axis=0, tiled=True)
-    hidden_all = lax.all_gather(hidden_hot, ("hot", "cold"), axis=1, tiled=True)
+    hidden_all = show_rails_by_axis(hidden_hot)
     hot_total = jnp.dot(hidden_all, down_cols, preferred_element_type=jnp.float32)
     cold_total = lax.psum_scatter(out_cold, "cold", scatter_dimension=1, tiled=True)
     total = hot_total + cold_total

time: 178 us -> 156 us (0.88)
  blocking collectives: 40.1 us -> 0 us
  waiting for transfers between devices: 93.3 us -> 103 us
  starting transfers between devices: 7.37 us -> 12.7 us
  matrix products: 16.5 us -> 18.7 us
    all_gather x1 -> x0, blocking collectives: 40.1 us -> none  [on_device(): hidden_all = lax.all_gather(hidden_hot, ('hot', 'cold'), axis=1, tiled=True)]
    ppermute x0 -> x5, waiting for transfers between devices: none -> 8.52 us  [start_the_ends(): lax.ppermute(x_new, comm_axis, [(h, h ^ g_now) for h in range(before)])]
    ppermute x0 -> x5, starting transfers between devices: none -> 8.48 us  [start_the_ends(): lax.ppermute(x_new, comm_axis, [(h, h ^ g_now) for h in range(before)])]
    all_to_all x1, starting transfers between devices: 7.32 us -> 4.17 us  [on_device(): lax.all_to_all(hot_down, ('hot', 'cold'), split_axis=1, concat_axis=0, ti...]
  transfers between devices with their start and end apart: 3 -> 8, of which waited for: 1 -> 5; matrix products, arithmetic and copies ran while one was open for 6% -> 3% of each run, Pallas kernels for 0% -> 0%
where the time goes in v1:
time: 156 us
  waiting for transfers between devices  103 us (66%)
  matrix products  18.7 us (12%)
  between operations  13.6 us (9%)
  starting transfers between devices  12.7 us (8%)
  other arithmetic  4.24 us (3%)
  local copies, waits for them, and re-layouts  3.66 us (2%)
    psum x1, waiting for transfers between devices, on_device(): gate_cold, up_cold = lax.psum((gate_part, up_part), 'hot')  94.4 us
    ppermute x5, waiting for transfers between devices, start_the_ends(): lax.ppermute(x_new, comm_axis, [(h, h ^ g_now) for h in range(before)])  8.52 us
    ppermute x5, starting transfers between devices, start_the_ends(): lax.ppermute(x_new, comm_axis, [(h, h ^ g_now) for h in range(before)])  8.48 us
    dot_general x1, matrix products, on_device(): out_cold = jnp.dot(hidden_cold, down_w, preferred_element_type=jnp.float32)  6.2 us
    dot_general x1, matrix products, on_device(): up_part = jnp.dot(normed_part, up_w, preferred_element_type=jnp.float32)  5.6 us
    all_to_all x1, starting transfers between devices, on_device(): lax.all_to_all(hot_down, ('hot', 'cold'), split_axis=1, concat_axis=0, ti...  4.17 us
    dot_general x1, matrix products, on_device(): gate_part = jnp.dot(normed_part, gate_w, preferred_element_type=jnp.float32)  3.23 us
  transfers between devices with their start and end apart: 8, of which 5 were waited for; matrix products, arithmetic and copies ran while one was open for 3% of the time, Pallas kernels for 0%

profile of v1, /device:TPU:0, one launch (start us, length us, event | category | flops | bytes accessed | tf_op | source)
XLA Modules:
  0.0 155.8 jit_solution(1884624153393103953)
XLA Ops:
  6.5 0.0 copy-start
  6.5 0.0 all-reduce.3.cloned.1.call-start
  6.5 1.6 %fusion = f32[64]{0:T(128)S(1)} fusion(bf16[64,8192]{1,0:T(8,128)(2,1)} %param.10), kind=kLoop, calls=%fused_computation.3 | loop fusion | flops 1572800 | bytes 1048832 | tf_op jit(solution)/shard_map/reduce_sum | solution.py:38
  8.1 2.5 %fusion.2 = bf16[64,8192]{1,0:T(8,128)(2,1)} fusion(bf16[64,8192]{1,0:T(8,128)(2,1)} %param.10, f32[8192]{0:T(1024)} %param.11, f32[64]{0:T(128)S(1)} %add_rsqrt_fusion), kind=kLoop, calls=%fused_computation.5 | loop fusion | flops 2097152 | bytes 2130176 | tf_op jit(solution)/shard_map/convert_element_type | solution.py:39
  10.7 0.0 slice-start
  10.7 0.0 slice-start.1
  10.7 5.6 %fusion.17 = f32[64,3584]{1,0:T(8,128)} fusion(bf16[1024,3584]{1,0:T(8,128)(2,1)} %param.17, bf16[64,8192]{1,0:T(8,128)(2,1)} %fusion.2, s32[]{:T(128)S(6)} %select_n.59), kind=kOutput, calls=%fused_computation.24 | convolution fusion | flops 469762048 | bytes 8388612 | tf_op jit(solution)/shard_map/dot_general | solution.py:57
  16.3 0.0 slice-done
  16.3 0.0 slice-done.1
  16.3 0.0 copy-start.4
  16.3 0.0 copy-start.5
  16.3 3.2 %fusion.19 = f32[64,3584]{1,0:T(8,128)} fusion(bf16[1024,3584]{1,0:T(8,128)(2,1)S(1)} %bitcast.24, bf16[64,8192]{1,0:T(8,128)(2,1)} %fusion.2, s32[]{:T(128)S(6)} %select_n.59), kind=kOutput, calls=%fused_computation.26 | convolution fusion | flops 469762048 | bytes 8388612 | tf_op jit(solution)/shard_map/dot_general | solution.py:56
  19.5 0.0 copy-start.1
  19.5 0.0 copy-start.2
  19.5 0.0 all-reduce.3.cloned.1.call-update
  19.5 0.0 copy-start.3
  19.5 0.0 reduce-scatter.2.cloned.1.call-start
  19.6 0.0 copy-done.4
  19.6 0.1 copy.16
  19.7 0.0 copy-done.5
  19.7 2.5 %scatter_custom_fusion = f32[14336]{0:T(1024)S(1)} fusion(s32[512]{0:T(512)S(1)} %compare_select_fusion, f32[512]{0:T(512)S(1)} %broadcast.20, f32[]{:T(128)} %constant.9.clone.1), kind=kCustom, calls=%fused_computation.30 | custom fusion | bytes 57348 | tf_op jit(solution)/shard_map/scatter | solution.py:49
  22.2 0.1 dynamic-slice_subtract_fusion
  22.3 0.0 copy-done
  22.3 1.6 %fusion.27 = f32[64,16]{0,1:T(8,128)S(1)} fusion(bf16[64,8192]{1,0:T(8,128)(2,1)} %fusion.2, bf16[16,8192]{1,0:T(8,128)(2,1)S(1)} %copy-done), kind=kOutput, calls=%fused_computation.41 | convolution fusion | flops 16777216 | bytes 1314816 | tf_op jit(solution)/shard_map/dot_general | solution.py:41
  23.9 94.4 %all-reduce.3.cloned.1.call-done = (f32[64,3584]{1,0:T(8,128)}, f32[64,3584]{1,0:T(8,128)}) async-done(((f32[64,3584]{1,0:T(8,128)}, f32[64,3584]{1,0:T(8,128)}), (f32[64,3584]{1,0:T(8,128)}, f32[64,3584]{1,0:T(8,128)})) %all-reduce.3.cloned.1.call-update) | async-done | bytes 1835024 | tf_op jit(solution)/shard_map/psum | solution.py:58
  118.3 0.3 mul.72
  118.6 6.2 %fusion.7 = f32[64,1024]{1,0:T(8,128)} fusion(bf16[3584,1024]{1,0:T(8,128)(2,1)} %param.18, f32[8,8,28,128]{3,2,1,0:T(8,128)S(1)} %bitcast.25, f32[64,3584]{1,0:T(8,128)} %get-tuple-element.5, f32[64,3584]{1,0:T(8,128)} %get-tuple-element.6, f32[3584]{0:T(1024)S(1)} %dynamic-slice_subtract_fusion), kind=kOutput, calls=%fused_computation.13 | convolution fusion | flops 471597056 | bytes 10369024 | tf_op jit(solution)/shard_map/dot_general | solution.py:60
  124.8 0.0 reduce-scatter.2.cloned.1.call-update
  124.8 0.0 copy-done.1
  124.9 0.0 copy-done.2
  124.9 0.4 fusion.4
  125.2 0.0 collective-permute-start
  125.3 0.0 copy-done.3
  125.3 0.7 copy.22
  126.0 4.2 %all-to-all-start = ((bf16[16,32,256]{2,0,1:T(8,128)(2,1)}), bf16[16,32,256]{2,0,1:T(8,128)(2,1)S(1)}, u32[]{:S(2)}, u32[]{:S(2)}) async-start(bf16[16,32,256]{2,0,1:T(8,128)(2,1)} %bitcast.22), calls=%async_computation | async-start | bytes 524288 | tf_op jit(solution)/shard_map/all_to_all | solution.py:61
  130.2 0.0 collective-permute-done
  130.2 1.8 %collective-permute-start.1 = (bf16[64,32]{0,1:T(8,128)(2,1)S(1)}, bf16[64,32]{0,1:T(8,128)(2,1)S(1)}, u32[]{:S(2)}, u32[]{:S(2)}) collective-permute-start(bf16[64,32]{0,1:T(8,128)(2,1)S(1)} %maximum_select_fusion.5), channel_id=1, source_target_pairs={{0,2},{1,3},{2,0},{3,1},{4,6},{5,7},{6,4},{7,5},{8,10},{9,11},{10,... | collective-permute-start | bytes 12296 | tf_op jit(solution)/shard_map/ppermute | solution.py:14
  132.0 2.0 %collective-permute-done.1 = bf16[64,32]{0,1:T(8,128)(2,1)S(1)} collective-permute-done((bf16[64,32]{0,1:T(8,128)(2,1)S(1)}, bf16[64,32]{0,1:T(8,128)(2,1)S(1)}, u32[]{:S(2)}, u32[]{:S(2)}) %collective-permute-start.1) | collective-permute-done | bytes 4128 | tf_op jit(solution)/shard_map/ppermute | solution.py:14
  134.0 1.9 %collective-permute-start.2 = (bf16[64,64]{0,1:T(8,128)(2,1)S(1)}, bf16[64,64]{0,1:T(8,128)(2,1)S(1)}, u32[]{:S(2)}, u32[]{:S(2)}) collective-permute-start(bf16[64,64]{0,1:T(8,128)(2,1)S(1)} %maximum_select_fusion.4), channel_id=1, source_target_pairs={{0,4},{1,5},{2,6},{3,7},{4,0},{5,1},{6,2},{7,3},{8,12},{9,13},{10,... | collective-permute-start | bytes 24584 | tf_op jit(solution)/shard_map/ppermute | solution.py:14
  135.9 2.1 %collective-permute-done.2 = bf16[64,64]{0,1:T(8,128)(2,1)S(1)} collective-permute-done((bf16[64,64]{0,1:T(8,128)(2,1)S(1)}, bf16[64,64]{0,1:T(8,128)(2,1)S(1)}, u32[]{:S(2)}, u32[]{:S(2)}) %collective-permute-start.2) | collective-permute-done | bytes 8224 | tf_op jit(solution)/shard_map/ppermute | solution.py:14
  138.0 1.9 %collective-permute-start.3 = (bf16[64,128]{0,1:T(8,128)(2,1)S(1)}, bf16[64,128]{0,1:T(8,128)(2,1)S(1)}, u32[]{:S(2)}, u32[]{:S(2)}) collective-permute-start(bf16[64,128]{0,1:T(8,128)(2,1)S(1)} %maximum_select_fusion.3), channel_id=1, source_target_pairs={{0,8},{1,9},{2,10},{3,11},{4,12},{5,13},{6,14},{7,15},{8,0},{9,1},... | collective-permute-start | bytes 49160 | tf_op jit(solution)/shard_map/ppermute | solution.py:14
  139.9 2.1 %collective-permute-done.3 = bf16[64,128]{0,1:T(8,128)(2,1)S(1)} collective-permute-done((bf16[64,128]{0,1:T(8,128)(2,1)S(1)}, bf16[64,128]{0,1:T(8,128)(2,1)S(1)}, u32[]{:S(2)}, u32[]{:S(2)}) %collective-permute-start.3) | collective-permute-done | bytes 16416 | tf_op jit(solution)/shard_map/ppermute | solution.py:14
  142.0 2.9 %collective-permute-start.4 = (bf16[64,256]{0,1:T(8,128)(2,1)S(1)}, bf16[64,256]{0,1:T(8,128)(2,1)S(1)}, u32[]{:S(2)}, u32[]{:S(2)}) collective-permute-start(bf16[64,256]{0,1:T(8,128)(2,1)S(1)} %maximum_select_fusion.2), channel_id=1, source_target_pairs={{0,16},{1,17},{2,18},{3,19},{4,20},{5,21},{6,22},{7,23},{8,24},{9,... | collective-permute-start | bytes 98312 | tf_op jit(solution)/shard_map/ppermute | solution.py:14
  145.0 2.3 %collective-permute-done.4 = bf16[64,256]{0,1:T(8,128)(2,1)S(1)} collective-permute-done((bf16[64,256]{0,1:T(8,128)(2,1)S(1)}, bf16[64,256]{0,1:T(8,128)(2,1)S(1)}, u32[]{:S(2)}, u32[]{:S(2)}) %collective-permute-start.4) | collective-permute-done | bytes 32800 | tf_op jit(solution)/shard_map/ppermute | solution.py:14
  147.3 0.0 all-to-all-done
  147.3 0.0 reduce-scatter.2.cloned.1.call-done
  147.3 1.7 %fusion.3 = bf16[64,256]{1,0:T(8,128)(2,1)} fusion(f32[64,256]{1,0:T(8,128)} %reduce-scatter.2.cloned.1.call-done, bf16[512,256]{1,0:T(8,128)(2,1)S(1)} %bitcast.27, bf16[64,256]{0,1:T(8,128)(2,1)S(1)} %collective-permute-done.4, bf16[64,256]{0,1:T(8,128)(2,1)S(1)} %maximum_select_fusion.2, pred[]{:T(512)S(6)} %eq.15), kind=kOutput, calls=%fused_computation.7 | convolution fusion | flops 17104896 | bytes 425985 | tf_op jit(solution)/shard_map/dot_general | solution.py:63
  (9 shorter events, 0.1 us)
Async XLA Ops:
  6.5 15.8 %copy-start = (bf16[16,8192]{1,0:T(8,128)(2,1)S(1)}, bf16[16,8192]{1,0:T(8,128)(2,1)}, u32[]{:S(2)}) copy-start(bf16[16,8192]{1,0:T(8,128)(2,1)} %param.12) | copy-start | bytes 786436
  6.5 111.8 %all-reduce.3.cloned.1.call-start = ((), (), s32[]{:S(2)}) async-start(), calls=%async_computation.3 | async-start | bytes 3670016 | tf_op jit(solution)/shard_map/psum | solution.py:58
  10.7 5.6 %slice-start = ((s8[7340032]{0:T(1024)(128)(4,1)}), s8[3145728]{0:T(1024)(128)(4,1)S(1)}, s32[]{:S(2)}) async-start(s8[7340032]{0:T(1024)(128)(4,1)} %bitcast.23), calls=%async_computation.4 | async-start | bytes 6291456
  10.7 5.6 %slice-start.1 = ((s8[7340032]{0:T(1024)(128)(4,1)}), s8[4194304]{0:T(1024)(128)(4,1)S(1)}, s32[]{:S(2)}) async-start(s8[7340032]{0:T(1024)(128)(4,1)} %bitcast.23), calls=%async_computation.5 | async-start | bytes 8388608
  16.3 3.3 %copy-start.4 = (s32[64,28]{0,1:T(8,128)S(1)}, s32[64,28]{0,1:T(8,128)}, u32[]{:S(2)}) copy-start(s32[64,28]{0,1:T(8,128)} %param.19) | copy-start | bytes 21508
  16.3 3.5 %copy-start.5 = (s32[512]{0:T(512)S(1)}, s32[512]{0:T(512)}, u32[]{:S(2)}) copy-start(s32[512]{0:T(512)} %param.15) | copy-start | bytes 6148
  19.5 105.3 %copy-start.1 = (bf16[64,8192]{1,0:T(8,128)(2,1)S(1)}, bf16[64,8192]{1,0:T(8,128)(2,1)}, u32[]{:S(2)}) copy-start(bf16[64,8192]{1,0:T(8,128)(2,1)} %fusion.2) | copy-start | bytes 3145732
  19.5 105.3 %copy-start.2 = (bf16[16,8192]{1,0:T(8,128)(2,1)S(1)}, bf16[16,8192]{1,0:T(8,128)(2,1)}, u32[]{:S(2)}) copy-start(bf16[16,8192]{1,0:T(8,128)(2,1)} %param.13) | copy-start | bytes 786436
  19.5 105.7 %copy-start.3 = (bf16[16,8192]{1,0:T(8,128)(2,1)S(1)}, bf16[16,8192]{1,0:T(8,128)(2,1)}, u32[]{:S(2)}) copy-start(bf16[16,8192]{1,0:T(8,128)(2,1)} %param.14) | copy-start | bytes 786436
  19.5 127.7 %reduce-scatter.2.cloned.1.call-start = ((), (), s32[]{:S(2)}) async-start(), calls=%async_computation.2 | async-start | bytes 327680 | tf_op jit(solution)/shard_map/reduce_scatter | solution.py:64
  125.2 4.9 %collective-permute-start = (bf16[64,16]{0,1:T(8,128)(2,1)S(1)}, bf16[64,16]{0,1:T(8,128)(2,1)S(1)}, u32[]{:S(2)}, u32[]{:S(2)}) collective-permute-start(bf16[64,16]{0,1:T(8,128)(2,1)S(1)} %fusion.4), channel_id=1, source_target_pairs={{0,1},{1,0},{2,3},{3,2},{4,5},{5,4},{6,7},{7,6},{8,9},{9,8},{10,11... | collective-permute-start | bytes 6152 | tf_op jit(solution)/shard_map/ppermute | solution.py:14
  126.0 21.3 %all-to-all-start = ((bf16[16,32,256]{2,0,1:T(8,128)(2,1)}), bf16[16,32,256]{2,0,1:T(8,128)(2,1)S(1)}, u32[]{:S(2)}, u32[]{:S(2)}) async-start(bf16[16,32,256]{2,0,1:T(8,128)(2,1)} %bitcast.22), calls=%async_computation | async-start | bytes 524288 | tf_op jit(solution)/shard_map/all_to_all | solution.py:61
  130.2 3.8 %collective-permute-start.1 = (bf16[64,32]{0,1:T(8,128)(2,1)S(1)}, bf16[64,32]{0,1:T(8,128)(2,1)S(1)}, u32[]{:S(2)}, u32[]{:S(2)}) collective-permute-start(bf16[64,32]{0,1:T(8,128)(2,1)S(1)} %maximum_select_fusion.5), channel_id=1, source_target_pairs={{0,2},{1,3},{2,0},{3,1},{4,6},{5,7},{6,4},{7,5},{8,10},{9,11},{10,... | collective-permute-start | bytes 12296 | tf_op jit(solution)/shard_map/ppermute | solution.py:14
  134.0 4.0 %collective-permute-start.2 = (bf16[64,64]{0,1:T(8,128)(2,1)S(1)}, bf16[64,64]{0,1:T(8,128)(2,1)S(1)}, u32[]{:S(2)}, u32[]{:S(2)}) collective-permute-start(bf16[64,64]{0,1:T(8,128)(2,1)S(1)} %maximum_select_fusion.4), channel_id=1, source_target_pairs={{0,4},{1,5},{2,6},{3,7},{4,0},{5,1},{6,2},{7,3},{8,12},{9,13},{10,... | collective-permute-start | bytes 24584 | tf_op jit(solution)/shard_map/ppermute | solution.py:14
  138.0 4.0 %collective-permute-start.3 = (bf16[64,128]{0,1:T(8,128)(2,1)S(1)}, bf16[64,128]{0,1:T(8,128)(2,1)S(1)}, u32[]{:S(2)}, u32[]{:S(2)}) collective-permute-start(bf16[64,128]{0,1:T(8,128)(2,1)S(1)} %maximum_select_fusion.3), channel_id=1, source_target_pairs={{0,8},{1,9},{2,10},{3,11},{4,12},{5,13},{6,14},{7,15},{8,0},{9,1},... | collective-permute-start | bytes 49160 | tf_op jit(solution)/shard_map/ppermute | solution.py:14
  142.0 5.2 %collective-permute-start.4 = (bf16[64,256]{0,1:T(8,128)(2,1)S(1)}, bf16[64,256]{0,1:T(8,128)(2,1)S(1)}, u32[]{:S(2)}, u32[]{:S(2)}) collective-permute-start(bf16[64,256]{0,1:T(8,128)(2,1)S(1)} %maximum_select_fusion.2), channel_id=1, source_target_pairs={{0,16},{1,17},{2,18},{3,19},{4,20},{5,21},{6,22},{7,23},{8,24},{9,... | collective-permute-start | bytes 98312 | tf_op jit(solution)/shard_map/ppermute | solution.py:14
Sparse Core Ops, SparseCore 0:
  19.7 98.5 all-reduce.2
  125.0 19.5 reduce-scatter.1
